TPU v7x, 32 devices: a whole 2x2x4 slice. The times are simulated.
32 devices in a mesh: row: 4 (over y, core), col: 8 (over z, x).
Axes of the slice: x: 2, y: 2, z: 4, core: 2. Of those that a mesh axis runs over, the one named last changes fastest.
Arguments:
- constraint: bfloat16 [8192, 16384], P('row', 'col'), may hold values from -0.046875 to 0.046875
- pattern: int32 [64, 128], P('row', 'col'), may hold values 0 or 1
- objective: float32 [16384, 256], P('col'), may hold values from -31 to 31
- row_bound: float32 [8192, 256], P('row'), may hold values from -31 to 31
- lower_bound: float32 [16384], P('col'), may hold values from -2 to -0.5
- upper_bound: float32 [16384], P('col'), may hold values from 0.5 to 2
Outputs:
- primal: float32 [16384, 256], P('col')
- dual_values: float32 [8192, 256], P('row')
- residual_norms: float32 [256], replicated
All inputs are finite; a program needn't handle non-finite values. No bound on the sum of `pattern` on one device may be relied on, other than what follows from the above.
Results may differ from a plain program's by a relative error of at most 0.0019.
Values may be sent and summed in bfloat16 or wider, within the bound.
No kernel may reach another device: no remote copies, remote signals or barrier semaphores. Data moves between devices by JAX's collectives and lax.ppermute only.
A program may use at most 128 MiB of HBM per device.

v0:
```python
import jax
import jax.numpy as jnp
from jax import lax
from jax.sharding import PartitionSpec as P

BLOCK = 128
ITERS = 3
step_primal = 0.6
step_dual = 0.6
epsilon = 1e-06


def masked(constraint, pattern):
    row_blocks, col_blocks = pattern.shape
    blocks = (
        constraint.reshape(row_blocks, BLOCK, col_blocks, BLOCK)
        * pattern.astype(jnp.bfloat16)[:, None, :, None]
    )
    return blocks.reshape(row_blocks * BLOCK, col_blocks * BLOCK)


def transposed(matrix, values):
    return lax.dot_general(
        matrix, values, (((0,), (0,)), ((), ())), preferred_element_type=jnp.float32
    )


def partial_stats(slack_share, displacement):
    return jnp.stack(
        [jnp.sum(jnp.maximum(slack_share, 0.0) ** 2, axis=0), jnp.sum(displacement**2, axis=0)]
    )


def settle(record):
    return lax.psum(record, ("row", "col"))


def on_device(constraint, pattern, objective, row_bound, lower_bound, upper_bound):
    matrix = masked(constraint, pattern)
    local_rows, local_cols = matrix.shape
    batch_size = objective.shape[1]
    row_devices = lax.axis_size("row")
    col_devices = lax.axis_size("col")
    total_rows = local_rows * row_devices
    total_cols = local_cols * col_devices
    row_share = local_rows // col_devices
    col_share = local_cols // row_devices
    row_offset = lax.axis_index("col") * row_share
    col_offset = lax.axis_index("row") * col_share
    records = []
    lower_share = lower_bound[:, None]
    upper_share = upper_bound[:, None]
    primal = jnp.zeros((local_cols, batch_size), jnp.float32)
    dual_values = jnp.zeros((local_rows, batch_size), jnp.float32)
    for iteration in range(ITERS):
        if iteration == 0:
            gradient = objective
        else:
            gradient = objective - lax.psum(
                transposed(matrix, dual_values.astype(jnp.bfloat16)), "row"
            )
        updated = jnp.clip(primal - step_primal * gradient, lower_share, upper_share)
        extrapolated = (2.0 * updated - primal).astype(jnp.bfloat16)
        product_rows = lax.psum(
            jnp.dot(matrix, extrapolated, preferred_element_type=jnp.float32), "col"
        )
        slack_rows = row_bound - product_rows
        dual_values = jnp.maximum(dual_values + step_dual * slack_rows, 0.0)
        slack_share = lax.dynamic_slice_in_dim(slack_rows, row_offset, row_share, 0)
        displacement = lax.dynamic_slice_in_dim(updated - primal, col_offset, col_share, 0)
        records.append(settle(partial_stats(slack_share, displacement)))
        primal = updated
    stacked = jnp.stack(records)
    residual_norms = jnp.zeros((batch_size,), jnp.float32)
    for iteration in range(ITERS):
        residual_norms = (
            residual_norms
            + jnp.sqrt(stacked[iteration, 0] / total_rows + epsilon)
            + jnp.sqrt(stacked[iteration, 1] / total_cols + epsilon)
        )
    return (primal, dual_values, residual_norms)


def solution(mesh):
    placed = (P("row", "col"), P("row", "col"), P("col", None), P("row", None), P("col"), P("col"))
    return jax.shard_map(
        on_device,
        mesh=mesh,
        in_specs=placed,
        out_specs=(P("col", None), P("row", None), P()),
        check_vma=False,
    )
```

profile of v0, /device:TPU:0, one launch (start us, length us, event | category | flops | bytes accessed | tf_op | source)
XLA Modules:
  0.0 529.3 jit_solution(18435655729704046118)
XLA Ops:
  7.2 0.0 all-reduce.7.cloned.1.call-start
  7.2 0.7 convert_element_type.18
  7.9 0.0 copy-start.6
  7.9 1.1 mul.45
  9.1 2.2 copy-done.6
  11.3 0.0 copy-start.8
  11.3 0.0 copy-start.11
  11.3 0.0 copy-start.12
  11.3 1.9 bitcast_multiply_fusion
  13.2 0.0 copy-start.7
  13.2 3.2 copy-done.7
  16.4 0.0 copy-done.8
  16.4 0.0 copy-done.11
  16.4 0.0 copy-done.12
  16.4 3.9 fusion.3
  20.3 0.0 copy-start
  20.3 0.0 all-reduce.7.cloned.1.call-update
  20.3 0.0 all-reduce.9.cloned.1.call-start
  20.4 105.1 %all-reduce.7.cloned.1.call-done = f32[2048,256]{1,0:T(8,128)} async-done(((f32[2048,256]{1,0:T(8,128)}), f32[2048,256]{1,0:T(8,128)}) %all-reduce.7.cloned.1.call-update) | async-done | bytes 2097168 | tf_op jit(solution)/shard_map/psum | solution.py:64
  125.5 0.0 copy-done
  125.5 1.9 sub.37
  127.4 0.0 copy-start.3
  127.4 1.4 copy-done.3
  128.8 7.2 %fusion.1 = f32[2048,256]{1,0:T(8,128)} fusion(bf16[2048,2048]{1,0:T(8,128)(2,1)} %copy-done.7, f32[2048,256]{1,0:T(8,128)S(1)} %sub.37), kind=kOutput, calls=%fused_computation.11 | convolution fusion | flops 2149056512 | bytes 12582912 | tf_op jit(solution)/shard_map/dot_general | solution.py:23
  136.0 0.0 all-reduce.9.cloned.1.call-update
  136.0 0.0 all-reduce.11.cloned.1.call-start
  136.1 50.8 %all-reduce.9.cloned.1.call-done = f32[2048,256]{1,0:T(8,128)} async-done(((f32[2048,256]{1,0:T(8,128)}), f32[2048,256]{1,0:T(8,128)}) %all-reduce.9.cloned.1.call-update) | async-done | bytes 2097168 | tf_op jit(solution)/shard_map/psum | solution.py:59
  186.9 0.0 copy-start.9
  186.9 2.7 maximum_minimum_fusion.1
  189.6 0.0 copy-start.1
  189.6 1.3 copy-done.1
  190.9 0.0 copy-done.9
  190.9 7.3 %fusion.4 = f32[2048,256]{1,0:T(8,128)} fusion(bf16[2048,2048]{1,0:T(8,128)(2,1)} %copy-done.7, f32[2048,256]{1,0:T(8,128)S(1)} %maximum_minimum_fusion.1, f32[2048,256]{1,0:T(8,128)S(1)} %copy-done.9, f32[2048]{0:T(1024)S(1)} %copy-done.11, f32[2048]{0:T(1024)S(1)} %copy-done.12), kind=kOutput, calls=%fused_computation.13 | convolution fusion | flops 2151153664 | bytes 14696448 | tf_op jit(solution)/shard_map/dot_general | solution.py:65
  198.2 0.0 all-reduce.11.cloned.1.call-update
  198.2 0.2 all-reduce.13.cloned.1.call-start
  198.5 102.3 %all-reduce.11.cloned.1.call-done = f32[2048,256]{1,0:T(8,128)} async-done(((f32[2048,256]{1,0:T(8,128)}), f32[2048,256]{1,0:T(8,128)}) %all-reduce.11.cloned.1.call-update) | async-done | bytes 2097168 | tf_op jit(solution)/shard_map/psum | solution.py:64
  300.7 0.0 copy-start.4
  300.7 2.0 sub.41
  302.7 0.0 copy-start.5
  302.8 1.3 copy-done.5
  304.0 0.0 copy-done.4
  304.0 7.3 %fusion.6 = f32[2048,256]{1,0:T(8,128)} fusion(bf16[2048,2048]{1,0:T(8,128)(2,1)} %copy-done.7, f32[2048,256]{1,0:T(8,128)S(1)} %sub.41, f32[2048,256]{1,0:T(8,128)S(1)} %copy-done.4), kind=kOutput, calls=%fused_computation.15 | convolution fusion | flops 2150629376 | bytes 14680064 | tf_op jit(solution)/shard_map/dot_general | solution.py:23
  311.3 0.0 all-reduce.13.cloned.1.call-update
  311.3 0.0 all-reduce.15.cloned.1.call-start
  311.4 50.8 %all-reduce.13.cloned.1.call-done = f32[2048,256]{1,0:T(8,128)} async-done(((f32[2048,256]{1,0:T(8,128)}), f32[2048,256]{1,0:T(8,128)}) %all-reduce.13.cloned.1.call-update) | async-done | bytes 2097168 | tf_op jit(solution)/shard_map/psum | solution.py:59
  362.2 0.0 copy-start.2
  362.2 4.4 maximum_minimum_fusion.2
  366.6 0.0 copy-start.10
  366.6 1.3 copy-done.10
  367.9 0.0 copy-done.2
  367.9 7.1 %fusion.5 = f32[2048,256]{1,0:T(8,128)} fusion(bf16[2048,2048]{1,0:T(8,128)(2,1)} %copy-done.7, f32[2048,256]{1,0:T(8,128)S(1)} %copy-done.2, f32[2048,256]{1,0:T(8,128)S(1)} %get-tuple-element.12), kind=kOutput, calls=%fused_computation.14 | convolution fusion | flops 2149056512 | bytes 14680064 | tf_op jit(solution)/shard_map/dot_general | solution.py:65
  375.0 0.0 all-reduce.15.cloned.1.call-update
  375.0 1.0 multiply_reduce_fusion.4
  376.0 1.0 multiply_reduce_fusion.3
  377.0 1.5 multiply_reduce_fusion.1
  378.5 99.0 %all-reduce.15.cloned.1.call-done = f32[2048,256]{1,0:T(8,128)} async-done(((f32[2048,256]{1,0:T(8,128)}), f32[2048,256]{1,0:T(8,128)}) %all-reduce.15.cloned.1.call-update) | async-done | bytes 2097168 | tf_op jit(solution)/shard_map/psum | solution.py:64
  477.5 4.9 add_maximum_fusion
  482.4 0.1 multiply_reduce_fusion.2
  482.4 39.8 %all-reduce = (f32[1,2,256]{2,1,0:T(2,128)S(1)}, f32[1,2,256]{2,1,0:T(2,128)S(1)}, f32[1,2,256]{2,1,0:T(2,128)S(1)}) all-reduce(f32[1,2,256]{2,1,0:T(2,128)S(1)} %maximum_bitcast_fusion.2, f32[1,2,256]{2,1,0:T(2,128)S(1)} %get-tuple-element.14, f32[1,2,256]{2,1,0:T(2,128)S(1)} %get-tuple-element.13), channel_id=1, replica_groups=mesh['row'=4,'col'=8] {'row','col'}, use_global_device_ids=true, to_apply=%region_13.14 | all-reduce | flops 1536 | bytes 12288 | tf_op jit(solution)/shard_map/psum | solution.py:35
  522.2 0.6 fusion.17
  (2 shorter events, 0.0 us)
Async XLA Ops:
  7.2 118.4 %all-reduce.7.cloned.1.call-start = ((), (), s32[]{:S(2)}) async-start(), calls=%async_computation | async-start | bytes 4194304 | tf_op jit(solution)/shard_map/psum | solution.py:64
  7.9 3.4 copy-start.6
  11.3 5.1 copy-start.8
  11.3 5.1 copy-start.11
  11.3 5.1 copy-start.12
  13.2 3.2 copy-start.7
  20.3 105.2 %copy-start = (f32[2048,256]{1,0:T(8,128)S(1)}, f32[2048,256]{1,0:T(8,128)}, u32[]{:S(2)}) copy-start(f32[2048,256]{1,0:T(8,128)} %param.9) | copy-start | bytes 6291460
  20.3 166.5 %all-reduce.9.cloned.1.call-start = ((), (), s32[]{:S(2)}) async-start(), calls=%async_computation.1 | async-start | bytes 4194304 | tf_op jit(solution)/shard_map/psum | solution.py:59
  127.4 1.4 copy-start.3
  136.0 164.7 %all-reduce.11.cloned.1.call-start = ((), (), s32[]{:S(2)}) async-start(), calls=%async_computation.2 | async-start | bytes 4194304 | tf_op jit(solution)/shard_map/psum | solution.py:64
  186.9 4.0 copy-start.9
  189.6 1.3 copy-start.1
  198.2 163.9 %all-reduce.13.cloned.1.call-start = ((), (), s32[]{:S(2)}) async-start(), calls=%async_computation.3 | async-start | bytes 4194304 | tf_op jit(solution)/shard_map/psum | solution.py:59
  300.7 3.3 copy-start.4
  302.7 1.3 copy-start.5
  311.3 166.1 %all-reduce.15.cloned.1.call-start = ((), (), s32[]{:S(2)}) async-start(), calls=%async_computation.4 | async-start | bytes 4194304 | tf_op jit(solution)/shard_map/psum | solution.py:64
  362.2 5.7 %copy-start.2 = (f32[2048,256]{1,0:T(8,128)S(1)}, f32[2048,256]{1,0:T(8,128)}, u32[]{:S(2)}) copy-start(f32[2048,256]{1,0:T(8,128)} %copy-done.1) | copy-start | bytes 6291460
  366.6 1.3 copy-start.10
Sparse Core Ops, SparseCore 0:
  20.5 105.0 all-reduce.6
  136.2 50.6 all-reduce.8
  198.3 102.3 all-reduce.10
  311.5 50.6 all-reduce.12
  375.1 102.3 all-reduce.14
where the time goes:
time: 530 us; the launch traced here: 529 us
  waiting for transfers between devices  408 us (77%)
  blocking collectives  39.8 us (8%)
  matrix products  32.8 us (6%)
  other arithmetic  22.6 us (4%)
  between operations  13.9 us (3%)
  local copies, waits for them, and re-layouts  11.9 us (2%)
    psum x3, waiting for transfers between devices, on_device(): lax.psum(jnp.dot(matrix, extrapolated, preferred_element_type=jnp.float32...  306 us
    psum x2, waiting for transfers between devices, on_device(): lax.psum(transposed(matrix, dual_values.astype(jnp.bfloat16)), 'row')  102 us
    psum x1, blocking collectives, settle(): return lax.psum(record, ('row', 'col'))  39.8 us
    dot_general x3, matrix products, on_device(): jnp.dot(matrix, extrapolated, preferred_element_type=jnp.float32)  18.3 us
    dot_general x2, matrix products, transposed(): lax.dot_general(matrix, values, (((0,), (0,)), ((), ())), preferred_eleme...  14.5 us
    unnamed x26, local copies, waits for them, and re-layouts  10.8 us
  transfers between devices with their start and end apart: 5, of which 5 were waited for; matrix products, arithmetic and copies ran while one was open for 1% of the time, Pallas kernels for 0%

commit v1 on v0

--- a/solution.py
+++ b/solution.py
@@ -61,8 +61,11 @@
             )
         updated = jnp.clip(primal - step_primal * gradient, lower_share, upper_share)
         extrapolated = (2.0 * updated - primal).astype(jnp.bfloat16)
-        product_rows = lax.psum(
-            jnp.dot(matrix, extrapolated, preferred_element_type=jnp.float32), "col"
+        product_rows = jnp.sum(
+            lax.all_gather(
+                jnp.dot(matrix, extrapolated, preferred_element_type=jnp.float32), "col"
+            ),
+            axis=0,
         )
         slack_rows = row_bound - product_rows
         dual_values = jnp.maximum(dual_values + step_dual * slack_rows, 0.0)

time: 530 us -> 927 us (1.75)
  waiting for transfers between devices: 408 us -> 781 us
  other arithmetic: 22.6 us -> 48.1 us
    all_gather x0 -> x3, waiting for transfers between devices: none -> 681 us  [on_device(): lax.all_gather(jnp.dot(matrix, extrapolated, preferred_element_type=jnp.f...]
    psum x3 -> x0, waiting for transfers between devices: 306 us -> none  [on_device(): lax.psum(jnp.dot(matrix, extrapolated, preferred_element_type=jnp.float32...]
    reduce_sum x0 -> x3, other arithmetic: none -> 25.5 us  [on_device(): jnp.sum(lax.all_gather(jnp.dot(matrix, extrapolated, preferred_element_ty...]
  transfers between devices with their start and end apart: 5 -> 5, of which waited for: 5 -> 5; matrix products, arithmetic and copies ran while one was open for 1% -> 0% of each run, Pallas kernels for 0% -> 0%
where the time goes in v1:
time: 927 us; the launch traced here: 926 us
  waiting for transfers between devices  781 us (84%)
  other arithmetic  48.1 us (5%)
  blocking collectives  38.5 us (4%)
  matrix products  32.8 us (4%)
  between operations  13.9 us (1%)
  local copies, waits for them, and re-layouts  11.9 us (1%)
    all_gather x3, waiting for transfers between devices, on_device(): lax.all_gather(jnp.dot(matrix, extrapolated, preferred_element_type=jnp.f...  681 us
    psum x2, waiting for transfers between devices, on_device(): lax.psum(transposed(matrix, dual_values.astype(jnp.bfloat16)), 'row')  99.3 us
    psum x1, blocking collectives, settle(): return lax.psum(record, ('row', 'col'))  38.5 us
    reduce_sum x3, other arithmetic, on_device(): jnp.sum(lax.all_gather(jnp.dot(matrix, extrapolated, preferred_element_ty...  25.5 us
  transfers between devices with their start and end apart: 5, of which 5 were waited for; matrix products, arithmetic and copies ran while one was open for 0% of the time, Pallas kernels for 0%

profile of v1, /device:TPU:0, one launch (start us, length us, event | category | flops | bytes accessed | tf_op | source)
XLA Modules:
  0.0 926.3 jit_solution(1521369840371373175)
XLA Ops:
  7.2 0.0 all-gather.7.cloned.1.call-start
  7.2 0.7 convert_element_type.18
  7.9 0.0 copy-start.6
  7.9 1.1 mul.45
  9.1 2.2 copy-done.6
  11.3 0.0 copy-start.8
  11.3 0.0 copy-start.11
  11.3 0.0 copy-start.12
  11.3 1.9 bitcast_multiply_fusion
  13.2 0.0 copy-start.7
  13.2 3.2 copy-done.7
  16.4 0.0 copy-done.8
  16.4 0.0 copy-done.11
  16.4 0.0 copy-done.12
  16.4 3.9 fusion.3
  20.3 0.0 all-gather.7.cloned.1.call-update
  20.3 0.0 all-reduce.4.cloned.1.call-start
  20.4 230.1 %all-gather.7.cloned.1.call-done = f32[16384,256]{1,0:T(8,128)} async-done(((f32[2048,256]{1,0:T(8,128)}), f32[16384,256]{1,0:T(8,128)}) %all-gather.7.cloned.1.call-update) | async-done | bytes 16777232 | tf_op jit(solution)/shard_map/all_gather | solution.py:65
  250.5 0.0 copy-start
  250.5 8.6 reduce_sum.81
  259.1 0.0 copy-done
  259.1 1.9 sub.37
  260.9 0.0 copy-start.3
  260.9 1.4 copy-done.3
  262.3 7.2 fusion.1
  269.6 0.0 all-reduce.4.cloned.1.call-update
  269.6 0.0 all-gather.9.cloned.1.call-start
  269.6 49.7 %all-reduce.4.cloned.1.call-done = f32[2048,256]{1,0:T(8,128)} async-done(((f32[2048,256]{1,0:T(8,128)}), f32[2048,256]{1,0:T(8,128)}) %all-reduce.4.cloned.1.call-update) | async-done | bytes 2097168 | tf_op jit(solution)/shard_map/psum | solution.py:59
  319.3 0.0 copy-start.9
  319.3 2.7 maximum_minimum_fusion.1
  322.0 0.0 copy-start.1
  322.0 1.3 copy-done.1
  323.3 0.0 copy-done.9
  323.3 7.3 fusion.4
  330.6 0.0 all-gather.9.cloned.1.call-update
  330.7 0.2 all-reduce.6.cloned.1.call-start
  330.9 227.3 %all-gather.9.cloned.1.call-done = f32[16384,256]{1,0:T(8,128)} async-done(((f32[2048,256]{1,0:T(8,128)}), f32[16384,256]{1,0:T(8,128)}) %all-gather.9.cloned.1.call-update) | async-done | bytes 16777232 | tf_op jit(solution)/shard_map/all_gather | solution.py:65
  558.2 8.5 reduce_sum.82
  566.6 0.0 copy-start.4
  566.6 2.0 sub.41
  568.6 0.0 copy-start.5
  568.7 1.3 copy-done.5
  569.9 0.0 copy-done.4
  569.9 7.3 fusion.6
  577.2 0.0 all-reduce.6.cloned.1.call-update
  577.2 0.0 all-gather.11.cloned.1.call-start
  577.3 49.7 %all-reduce.6.cloned.1.call-done = f32[2048,256]{1,0:T(8,128)} async-done(((f32[2048,256]{1,0:T(8,128)}), f32[2048,256]{1,0:T(8,128)}) %all-reduce.6.cloned.1.call-update) | async-done | bytes 2097168 | tf_op jit(solution)/shard_map/psum | solution.py:59
  627.0 0.0 copy-start.2
  627.0 4.4 maximum_minimum_fusion.2
  631.4 0.0 copy-start.10
  631.4 1.3 copy-done.10
  632.7 0.0 copy-done.2
  632.7 7.1 fusion.5
  639.8 0.0 all-gather.11.cloned.1.call-update
  639.8 1.0 multiply_reduce_fusion.4
  640.8 1.0 multiply_reduce_fusion.3
  641.8 1.5 multiply_reduce_fusion.1
  643.3 224.0 %all-gather.11.cloned.1.call-done = f32[16384,256]{1,0:T(8,128)} async-done(((f32[2048,256]{1,0:T(8,128)}), f32[16384,256]{1,0:T(8,128)}) %all-gather.11.cloned.1.call-update) | async-done | bytes 16777232 | tf_op jit(solution)/shard_map/all_gather | solution.py:65
  867.3 8.5 reduce_sum.83
  875.7 4.9 add_maximum_fusion
  880.6 0.1 multiply_reduce_fusion.2
  880.7 38.5 %all-reduce = (f32[1,2,256]{2,1,0:T(2,128)S(1)}, f32[1,2,256]{2,1,0:T(2,128)S(1)}, f32[1,2,256]{2,1,0:T(2,128)S(1)}) all-reduce(f32[1,2,256]{2,1,0:T(2,128)S(1)} %maximum_bitcast_fusion.2, f32[1,2,256]{2,1,0:T(2,128)S(1)} %get-tuple-element.14, f32[1,2,256]{2,1,0:T(2,128)S(1)} %get-tuple-element.13), channel_id=1, replica_groups=mesh['row'=4,'col'=8] {'row','col'}, use_global_device_ids=true, to_apply=%region_13.14 | all-reduce | flops 1536 | bytes 12288 | tf_op jit(solution)/shard_map/psum | solution.py:35
  919.1 0.6 fusion.17
  (2 shorter events, 0.0 us)
Async XLA Ops:
  7.2 243.3 %all-gather.7.cloned.1.call-start = ((), (), s32[]{:S(2)}) async-start(), calls=%async_computation.2 | async-start | bytes 18874368 | tf_op jit(solution)/shard_map/all_gather | solution.py:65
  7.9 3.4 copy-start.6
  11.3 5.1 copy-start.8
  11.3 5.1 copy-start.11
  11.3 5.1 copy-start.12
  13.2 3.2 copy-start.7
  20.3 299.0 %all-reduce.4.cloned.1.call-start = ((), (), s32[]{:S(2)}) async-start(), calls=%async_computation | async-start | bytes 4194304 | tf_op jit(solution)/shard_map/psum | solution.py:59
  250.5 8.6 copy-start
  260.9 1.4 copy-start.3
  269.6 288.6 %all-gather.9.cloned.1.call-start = ((), (), s32[]{:S(2)}) async-start(), calls=%async_computation.3 | async-start | bytes 18874368 | tf_op jit(solution)/shard_map/all_gather | solution.py:65
  319.3 4.0 copy-start.9
  322.0 1.3 copy-start.1
  330.7 296.3 %all-reduce.6.cloned.1.call-start = ((), (), s32[]{:S(2)}) async-start(), calls=%async_computation.1 | async-start | bytes 4194304 | tf_op jit(solution)/shard_map/psum | solution.py:59
  566.6 3.3 copy-start.4
  568.6 1.3 copy-start.5
  577.2 290.0 %all-gather.11.cloned.1.call-start = ((), (), s32[]{:S(2)}) async-start(), calls=%async_computation.4 | async-start | bytes 18874368 | tf_op jit(solution)/shard_map/all_gather | solution.py:65
  627.0 5.7 copy-start.2
  631.4 1.3 copy-start.10
Sparse Core Ops, SparseCore 0:
  20.5 229.9 all-gather.6
  269.7 49.5 all-reduce.3
  330.8 227.3 all-gather.8
  577.4 49.5 all-reduce.5
  639.9 227.3 all-gather.10
